TPU v7x, 256 devices: a whole 4x4x8 slice. The times are simulated.
256 devices in a mesh: dp: 8 (over z_hi, core), tensor: 32 (over x, y, z_lo).
Axes of the slice: x: 4, y: 4, z: 8 (z_hi: 4, z_lo: 2; z = z_hi * 2 + z_lo), core: 2. Of those that a mesh axis runs over, the one named last changes fastest.
Arguments:
- inputs: bfloat16 [6144, 6144], P(('dp', 'tensor')), may hold values from -0.29882812 to 0.29882812
- norm_gain: float32 [6144], replicated, may hold values from 0.1 to 1.9
- norm_bias: float32 [6144], replicated, may hold values from -3 to 3
- query_grad: bfloat16 [6144, 12288], P('dp', 'tensor'), may hold values from -0.119628906 to 0.119628906
- stream_grad: bfloat16 [6144, 6144], P(('dp', 'tensor')), may hold values from -2.390625 to 2.390625
- query_weight: bfloat16 [6144, 12288], P(None, 'tensor'), may hold values from -0.0546875 to 0.0546875
Outputs:
- input_grad: bfloat16 [6144, 6144], P(('dp', 'tensor'))
- weight_grad: bfloat16 [6144, 12288], P(None, 'tensor')
All inputs are finite; a program needn't handle non-finite values.
Results may differ from a plain program's by a relative error of at most 0.019.
Values may be sent and summed in bfloat16 or wider, within the bound.
A program may use at most 128 MiB of HBM per device.

v0:
```python
import jax
import jax.numpy as jnp
from jax import lax
from jax.sharding import Mesh
from jax.sharding import PartitionSpec as P

TENSOR = ("tensor_0", "tensor_1", "tensor_2")
DP_TENSOR = ("dp", "tensor_0", "tensor_1", "tensor_2")


epsilon = 1e-05


def sum_by_axis(terms, axes):
    running = terms.astype(jnp.bfloat16)
    for axis in axes:
        running = lax.psum_scatter(running, axis, scatter_dimension=0, tiled=True)
    return running.astype(jnp.float32)


def normalize(values, norm_gain, norm_bias):
    as_float = values.astype(jnp.float32)
    centre = jnp.mean(as_float, axis=-1, keepdims=True)
    offsets = as_float - centre
    variance = jnp.mean(offsets * offsets, axis=-1, keepdims=True)
    inverse = lax.rsqrt(variance + epsilon)
    scaled = offsets * inverse
    normed = (scaled * norm_gain + norm_bias).astype(jnp.bfloat16)
    return (scaled, inverse, normed)


def norm_backward(scaled, inverse, normed_grad, norm_gain, stream_grad):
    weighted = normed_grad * norm_gain
    first_moment = jnp.mean(weighted, axis=-1, keepdims=True)
    second_moment = jnp.mean(weighted * scaled, axis=-1, keepdims=True)
    result = stream_grad.astype(jnp.float32) + inverse * (
        weighted - first_moment - scaled * second_moment
    )
    return result.astype(jnp.bfloat16)


def shards(inputs, norm_gain, norm_bias, query_grad, stream_grad, query_weight):
    scaled, inverse, normed = normalize(inputs, norm_gain, norm_bias)
    unused_scaled, unused_inverse, piece_normed = normalize(
        lax.all_gather(inputs, TENSOR, axis=0, tiled=True), norm_gain, norm_bias
    )
    grad_rows = query_grad
    weight_grad = lax.psum(
        lax.dot_general(
            piece_normed, grad_rows, (((0,), (0,)), ((), ())), preferred_element_type=jnp.float32
        ).astype(jnp.bfloat16),
        "dp",
    )
    grad_rows = query_grad
    normed_grad = sum_by_axis(
        lax.dot_general(
            grad_rows, query_weight, (((1,), (1,)), ((), ())), preferred_element_type=jnp.float32
        ),
        TENSOR,
    )
    input_grad = norm_backward(scaled, inverse, normed_grad, norm_gain, stream_grad)
    return (input_grad, weight_grad)


def solution(mesh):
    torus = Mesh(
        mesh.devices.reshape(mesh.shape["dp"], 4, 4, 2), ("dp", "tensor_0", "tensor_1", "tensor_2")
    )
    return jax.shard_map(
        shards,
        mesh=torus,
        in_specs=(
            P(DP_TENSOR, None),
            P(),
            P(),
            P("dp", TENSOR),
            P(DP_TENSOR, None),
            P(None, TENSOR),
        ),
        out_specs=(P(DP_TENSOR, None), P(None, TENSOR)),
        check_vma=False,
    )
```

profile of v0, /device:TPU:1, one launch (start us, length us, event | category | flops | bytes accessed | tf_op | source)
XLA Modules:
  0.0 391.3 jit_solution(754662459261700142)
XLA Ops:
  8.0 0.0 reduce-scatter.4.cloned.1.call-start
  8.1 1.0 copy-done
  9.1 9.8 %convolution_convert_fusion = bf16[768,6144]{1,0:T(8,128)(2,1)} fusion(bf16[768,384]{1,0:T(8,128)(2,1)S(1)} %copy-done, bf16[6144,384]{1,0:T(8,128)(2,1)} %param.11), kind=kOutput, calls=%fused_computation.8 | convolution fusion | flops 3628597248 | bytes 14745600 | tf_op jit(solution)/shard_map/dot_general | solution.py:56
  18.8 0.0 all-gather.2.cloned.1.call-start
  18.9 0.5 all-gather.2.cloned.1.call-update
  19.4 0.0 reduce-scatter.6.cloned.1.call-start
  19.5 94.8 %reduce-scatter.4.cloned.1.call-done = bf16[192,6144]{1,0:T(8,128)(2,1)} async-done(((bf16[768,6144]{1,0:T(8,128)(2,1)}), bf16[192,6144]{1,0:T(8,128)(2,1)}) %reduce-scatter.4.cloned.1.call-update) | async-done | bytes 2359312 | tf_op jit(solution)/shard_map/reduce_scatter | solution.py:17
  114.3 0.0 reduce-scatter.8.cloned.1.call-start
  114.4 124.1 %all-gather.2.cloned.1.call-done = bf16[768,6144]{1,0:T(8,128)(2,1)} async-done(((bf16[24,6144]{1,0:T(8,128)(2,1)}), bf16[768,6144]{1,0:T(8,128)(2,1)}) %all-gather.2.cloned.1.call-update) | async-done | bytes 9437200 | tf_op jit(solution)/shard_map/all_gather | solution.py:45
  238.5 5.3 %convert_reduce_fusion = f32[768]{0:T(1024)S(1)} fusion(bf16[768,6144]{1,0:T(8,128)(2,1)} %all-gather.2.cloned.1.call-done), kind=kLoop, calls=%fused_computation.1 | loop fusion | flops 9436416 | bytes 9440256 | tf_op jit(solution)/shard_map/reduce_sum | solution.py:23
  243.8 1.2 copy-done.1
  245.0 2.6 fusion.2
  247.6 0.0 reduce-scatter.6.cloned.1.call-done
  247.6 0.0 reduce-scatter.8.cloned.1.call-update
  247.6 0.0 all-reduce.2.cloned.1.call-start
  247.7 10.0 %fusion.12 = bf16[6144,384]{1,0:T(8,128)(2,1)} fusion(bf16[768,384]{1,0:T(8,128)(2,1)S(1)} %copy-done, bf16[768,6144]{1,0:T(8,128)(2,1)} %all-gather.2.cloned.1.call-done, f32[6144]{0:T(1024)S(1)} %copy-done.5, f32[6144]{0:T(1024)S(1)} %copy-done.4, f32[768]{0:T(1024)S(1)} %add_rsqrt_fusion, f32[768]{0:T(1024)S(1)} %broadcast_multiply_fusion), kind=kOutput, calls=%fused_computation.14 | convolution fusion | flops 3654549504 | bytes 14800896 | tf_op jit(solution)/shard_map/dot_general | solution.py:49
  257.7 0.0 all-reduce.2.cloned.1.call-update
  257.7 0.2 convert_reduce_fusion.1
  257.9 0.3 fusion.24
  258.2 7.8 %reduce-scatter.8.cloned.1.call-done = bf16[24,6144]{1,0:T(8,128)(2,1)} async-done(((bf16[48,6144]{1,0:T(8,128)(2,1)}), bf16[24,6144]{1,0:T(8,128)(2,1)}) %reduce-scatter.8.cloned.1.call-update) | async-done | bytes 294928 | tf_op jit(solution)/shard_map/reduce_scatter | solution.py:17
  266.0 1.2 fusion.25
  267.3 2.0 fusion.23
  269.2 110.0 %all-reduce.2.cloned.1.call-done = bf16[6144,384]{1,0:T(8,128)(2,1)} async-done(((bf16[6144,384]{1,0:T(8,128)(2,1)}), bf16[6144,384]{1,0:T(8,128)(2,1)}) %all-reduce.2.cloned.1.call-update) | async-done | bytes 4718608 | tf_op jit(solution)/shard_map/psum | solution.py:48
  379.2 5.0 %copy.9 = bf16[6144,384]{1,0:T(8,128)(2,1)} copy(bf16[6144,384]{1,0:T(8,128)(2,1)} %all-reduce.2.cloned.1.call-done) | data formatting | bytes 9437184
  (17 shorter events, 0.1 us)
Async XLA Ops:
  8.0 1.1 copy-start
  8.0 106.3 %reduce-scatter.4.cloned.1.call-start = ((), (), s32[]{:S(2)}) async-start(), calls=%async_computation.3 | async-start | bytes 11796480 | tf_op jit(solution)/shard_map/reduce_scatter | solution.py:17
  18.8 219.6 %all-gather.2.cloned.1.call-start = ((), (), s32[]{:S(2)}) async-start(), calls=%async_computation.6 | async-start | bytes 9732096 | tf_op jit(solution)/shard_map/all_gather | solution.py:45
  19.4 228.1 %reduce-scatter.6.cloned.1.call-start = ((), (), s32[]{:S(2)}) async-start(), calls=%async_computation.4 | async-start | bytes 2949120 | tf_op jit(solution)/shard_map/reduce_scatter | solution.py:17
  114.3 133.4 %copy-start.4 = (f32[6144]{0:T(1024)S(1)}, f32[6144]{0:T(1024)}, u32[]{:S(2)}) copy-start(f32[6144]{0:T(1024)} %param.7) | copy-start | bytes 73732
  114.3 133.4 %copy-start.5 = (f32[6144]{0:T(1024)S(1)}, f32[6144]{0:T(1024)}, u32[]{:S(2)}) copy-start(f32[6144]{0:T(1024)} %param.8) | copy-start | bytes 73732
  114.3 151.7 %reduce-scatter.8.cloned.1.call-start = ((), (), s32[]{:S(2)}) async-start(), calls=%async_computation.5 | async-start | bytes 884736 | tf_op jit(solution)/shard_map/reduce_scatter | solution.py:17
  238.5 6.5 %copy-start.1 = (bf16[768,6144]{1,0:T(8,128)(2,1)S(1)}, bf16[768,6144]{1,0:T(8,128)(2,1)}, u32[]{:S(2)}) copy-start(bf16[768,6144]{1,0:T(8,128)(2,1)} %all-gather.2.cloned.1.call-done) | copy-start | bytes 28311556
  247.6 10.1 %copy-start.2 = (bf16[24,6144]{1,0:T(8,128)(2,1)S(1)}, bf16[24,6144]{1,0:T(8,128)(2,1)}, u32[]{:S(2)}) copy-start(bf16[24,6144]{1,0:T(8,128)(2,1)} %param.6) | copy-start | bytes 884740
  247.6 19.6 %copy-start.3 = (bf16[24,6144]{1,0:T(8,128)(2,1)S(1)}, bf16[24,6144]{1,0:T(8,128)(2,1)}, u32[]{:S(2)}) copy-start(bf16[24,6144]{1,0:T(8,128)(2,1)} %param.10) | copy-start | bytes 884740
  247.6 131.6 %all-reduce.2.cloned.1.call-start = ((), (), s32[]{:S(2)}) async-start(), calls=%async_computation.7 | async-start | bytes 9437184 | tf_op jit(solution)/shard_map/psum | solution.py:48
Sparse Core Ops, SparseCore 0:
  19.0 95.2 reduce-scatter.3
  116.9 124.3 reduce-scatter.5
  247.7 18.2 reduce-scatter.7
Sparse Core Ops, SparseCore 1:
  21.1 217.3 all-gather.1
  257.8 121.4 all-reduce.1
where the time goes:
time: 395 us; the launch traced here: 391 us
  waiting for transfers between devices  337 us (85%)
  matrix products  19.8 us (5%)
  between operations  15.3 us (4%)
  other arithmetic  11.5 us (3%)
  local copies, waits for them, and re-layouts  7.22 us (2%)
    all_gather x1, waiting for transfers between devices, shards(): lax.all_gather(inputs, TENSOR, axis=0, tiled=True)  124 us
    psum x1, waiting for transfers between devices, shards(): lax.psum(lax.dot_general(piece_normed, grad_rows, (((0,), (0,)), ((), ())...  110 us
    reduce_scatter x3, waiting for transfers between devices, sum_by_axis(): running = lax.psum_scatter(running, axis, scatter_dimension=0, tiled=True)  103 us
    dot_general x1, matrix products, shards(): lax.dot_general(piece_normed, grad_rows, (((0,), (0,)), ((), ())), prefer...  10 us
    dot_general x1, matrix products, shards(): lax.dot_general(grad_rows, query_weight, (((1,), (1,)), ((), ())), prefer...  9.76 us
  transfers between devices with their start and end apart: 5, of which 4 were waited for; matrix products, arithmetic and copies ran while one was open for 6% of the time, Pallas kernels for 0%

commit v1 on v0

v1 whole, which is shorter than its diff:
```python
import jax
import jax.numpy as jnp
from jax import lax
from jax.experimental import pallas as pl
from jax.experimental.pallas import tpu as pltpu
from jax.sharding import Mesh
from jax.sharding import PartitionSpec as P

MESH = pl.DeviceIdType.MESH
DP = ("zh", "c")
TENSOR = ("x", "y", "zl")
ALL = DP + TENSOR
EPS = 1e-05

F32 = jnp.float32
BF16 = jnp.bfloat16


def kernel(
    x_ref, gain_ref, bias_ref, q_ref, stream_ref, w_ref, dx_ref, dw_ref,
    scaled, inverse, normed, spread, own, xs, xt, qs, ws, wrelay, gs, rsb, fin, out,
    tsend, trecv, tsum, tzs, tzr, back, ngf,
    send_sem, recv_sem, local_sem,
):
    zh, c, x, y, zl = [lax.axis_index(name) for name in ALL]
    tok, width = x_ref.shape
    block = width // 8
    cols = q_ref.shape[1]
    rows_yz = 4 * tok
    group = 8 * rows_yz
    sub = block // 3
    quarter = block // 4

    def wrap(value):
        return lax.rem(value + 8, 4)

    xm, xp, xo = wrap(x - 1), wrap(x + 1), wrap(x + 2)
    ym, yp, yo = wrap(y - 1), wrap(y + 1), wrap(y + 2)
    zm, zp = wrap(zh - 1), wrap(zh + 1)
    other = 1 - c

    def at(offset, size, unit):
        return pl.ds(pl.multiple_of(offset, unit), size)

    copies = []
    locals_ = []

    def send(src, dst, **where):
        i = len(copies)
        copy = pltpu.make_async_remote_copy(
            src_ref=src,
            dst_ref=dst,
            send_sem=send_sem.at[i],
            recv_sem=recv_sem.at[i],
            device_id=where,
            device_id_type=MESH,
        )
        copy.start()
        copies.append(copy)
        return copy

    def local(src, dst):
        copy = pltpu.make_async_copy(src, dst, local_sem.at[len(locals_)])
        copy.start()
        locals_.append(copy)
        return copy

    pairs = [(dc, dx) for dc in range(2) for dx in range(4) if dc or dx]
    barrier = pltpu.get_barrier_semaphore()
    partners = [{"x": wrap(x + dx), "c": lax.rem(c + dc, 2)} for dc, dx in pairs]
    partners += [{"y": yp}, {"y": ym}, {"zl": 1 - zl}, {"zh": zp}, {"zh": zm}]
    for where in partners:
        pl.semaphore_signal(barrier, inc=1, device_id=where, device_id_type=MESH)

    mine = x * 2 + c
    q_local = local(q_ref, qs.at[0, c])
    w_local = local(w_ref.at[at(mine * block, block, block), :], ws.at[0])

    values = x_ref[...].astype(F32)
    centre = jnp.mean(values, axis=-1, keepdims=True)
    offsets = values - centre
    variance = jnp.mean(offsets * offsets, axis=-1, keepdims=True)
    inv = lax.rsqrt(variance + EPS)
    inverse[...] = jnp.broadcast_to(inv, inverse.shape)
    scaled[...] = offsets * inv
    normed[...] = (scaled[...] * gain_ref[...] + bias_ref[...]).astype(BF16)

    pl.semaphore_wait(barrier, len(partners))

    spread_in = []
    for dc, dx in pairs:
        tx, tc = wrap(x + dx), lax.rem(c + dc, 2)
        spread_in.append(
            send(normed.at[:, at((tx * 2 + tc) * block, block, 128)], spread.at[c * 4 + x], x=tx, c=tc)
        )
    q_d2d = {0: send(q_ref, qs.at[0, c], c=other)}
    q_down = send(q_ref, qs.at[1, c], x=xm)
    q_up = send(q_ref, qs.at[3, c], x=xp)

    spread[c * 4 + x] = normed[:, at(mine * block, block, 128)]
    for copy in spread_in:
        copy.wait_recv()
    for g in range(2):
        own[g] = jnp.concatenate([spread[g * 4 + i].astype(F32) for i in range(4)], axis=0).astype(BF16)
    base = y * 2 + zl
    own_in = local(own, xs.at[:, at(base * rows_yz, rows_yz, rows_yz), :])
    sl = [pl.ds(j * sub, sub) for j in range(3)]
    zl_in = [send(own.at[:, :, sl[j]], xs.at[:, at(base * rows_yz, rows_yz, rows_yz), sl[j]], zl=1 - zl) for j in range(3)]

    def w_rows(i, begin=0, size=block):
        return w_ref.at[at((i * 2 + c) * block + begin, size, size), :]

    w_down = send(w_rows(xm), ws.at[1], x=xm)
    w_up = send(w_rows(xp), ws.at[3], x=xp)
    half_w = block // 2
    w_relay_up = send(w_rows(xo, 0, half_w), wrelay.at[0], x=xp)
    w_relay_down = send(w_rows(xo, half_w, half_w), wrelay.at[1], x=xm)

    own_in.wait()
    y_up, y_down, relay_up, relay_down = {}, {}, {}, {}

    def y_rows(i):
        return at(i * 2 * rows_yz, 2 * rows_yz, 2 * rows_yz)

    def y_first(j):
        zl_in[j].wait_recv()
        piece = xs.at[:, y_rows(y), sl[j]]
        y_up[j] = send(piece, piece, y=yp)
        y_down[j] = send(piece, piece, y=ym)

    def y_relay(j):
        y_up[j].wait_recv()
        piece = xs.at[0, y_rows(ym), sl[j]]
        relay_up[j] = send(piece, piece, y=yp)
        y_down[j].wait_recv()
        piece = xs.at[1, y_rows(yp), sl[j]]
        relay_down[j] = send(piece, piece, y=ym)

    units = [(0, 0), (0, 1), (0, 2), (1, None), (3, None), (2, None)]

    def geometry(u):
        k, j = units[u]
        if j is None:
            return k, 0, quarter, 0
        return k, j * sub, sub // 4, j * (sub // 8)

    def g_rows(u, q, h):
        k, begin, step, _ = geometry(u)
        return at(begin + q * step + h * (step // 2), step // 2, 16)

    ring = {}

    def product(u):
        k, j = units[u]
        if j is not None:
            relay_up[j].wait_recv()
            relay_down[j].wait_recv()
            for g in range(2):
                xt[g, pl.ds(j * sub, sub), :] = xs[g, :, pl.ds(j * sub, sub)].T
            if j == 0:
                q_local.wait()
            if j == 0:
                q_d2d[0].wait_recv()
            pieces = [j * sub]
        else:
            q_d2d[k].wait_recv()
            pieces = [0, sub, 2 * sub]
        for begin in pieces:
            rows = pl.ds(begin, sub)
            gs[k, rows, :] = (
                jnp.dot(xt[0, rows, :], qs[k, 0], preferred_element_type=F32)
                + jnp.dot(xt[1, rows, :], qs[k, 1], preferred_element_type=F32)
            ).astype(BF16)

    def slot(u, d, s):
        k, _, step, r0 = geometry(u)
        return rsb.at[k, d, s, pl.ds(r0, step // 2), :]

    def rs_step(u, s):
        k = units[u][0]
        for d, (peer, sign) in enumerate(((zp, -1), (zm, 1))):
            if s == 0:
                ring[u, d, 0] = send(gs.at[k, g_rows(u, wrap(zh + sign), d), :], slot(u, d, 0), zh=peer)
                continue
            ring[u, d, s - 1].wait_recv()
            mine_part = gs[k, g_rows(u, wrap(zh + sign * (s + 1)), d), :].astype(F32)
            here = slot(u, d, s - 1)
            total = (here[...].astype(F32) + mine_part).astype(BF16)
            if s < 3:
                here[...] = total
                ring[u, d, s] = send(here, slot(u, d, s), zh=peer)
            elif k == 0:
                out[out_rows(u, 0, zh, d), :] = total
            else:
                fin[k, pl.ds(d * (quarter // 2), quarter // 2), :] = total
        if s == 3 and k:
            far = wrap(x + k)
            step = geometry(u)[2]
            ring[u, "x"] = send(fin.at[k], out.at[at(mine * block + zh * step, step, step), :], x=far)

    def source(k):
        return wrap(x - k) * 2 + c

    def out_rows(u, k, q, h):
        _, begin, step, _ = geometry(u)
        return at(source(k) * block + begin + q * step + h * (step // 2), step // 2, 16)

    def ag_step(u, s):
        k = units[u][0]
        if s == 0 and k:
            ring[u, "x"].wait_recv()
        for d, (peer, sign) in enumerate(((zp, -1), (zm, 1))):
            if s:
                ring[u, d, "a", s - 1].wait_recv()
            if s < 3:
                rows = out.at[out_rows(u, k, wrap(zh + sign * s), d), :]
                ring[u, d, "a", s] = send(rows, rows, zh=peer)
        if s == 3:
            size = sub if units[u][1] is not None else block
            begin = geometry(u)[1]
            whole = at(source(k) * block + begin, size, 16)
            ring[u, "c"] = send(out.at[whole, :], out.at[whole, :], c=other)
            local(out.at[whole, :], dw_ref.at[whole, :])

    def finish(u):
        k = units[u][0]
        ring[u, "c"].wait_recv()
        size = sub if units[u][1] is not None else block
        begin = geometry(u)[1]
        whole = at((wrap(x - k) * 2 + other) * block + begin, size, 16)
        local(out.at[whole, :], dw_ref.at[whole, :])

    q_relay = {}

    def q_forward():
        half = group // 2
        q_down.wait_recv()
        q_relay["down"] = send(qs.at[1, c, pl.ds(0, half), :], qs.at[2, c, pl.ds(0, half), :], x=xm)
        q_d2d[1] = send(qs.at[1, c], qs.at[1, c], c=other)
        q_up.wait_recv()
        q_relay["up"] = send(qs.at[3, c, pl.ds(half, half), :], qs.at[2, c, pl.ds(half, half), :], x=xp)
        q_d2d[3] = send(qs.at[3, c], qs.at[3, c], c=other)

    def q_last():
        q_relay["down"].wait_recv()
        q_relay["up"].wait_recv()
        q_d2d[2] = send(qs.at[2, c], qs.at[2, c], c=other)

    w_second = {}

    def w_forward():
        w_relay_up.wait_recv()
        w_second["up"] = send(wrelay.at[0], ws.at[2, pl.ds(0, half_w), :], x=xp)
        w_relay_down.wait_recv()
        w_second["down"] = send(wrelay.at[1], ws.at[2, pl.ds(half_w, half_w), :], x=xm)

    term_sent = {}

    def terms(dy):
        if dy == 2:
            w_local.wait()
            w_down.wait_recv()
            w_up.wait_recv()
            w_second["up"].wait_recv()
            w_second["down"].wait_recv()
        part = block // 3
        for g in range(2):
            for n in range(3):
                total = None
                for k in range(4):
                    piece = lax.dot_general(
                        qs[k, g, y_rows(wrap(y + dy)), :],
                        ws[k, pl.ds(n * part, part), :],
                        (((1,), (1,)), ((), ())),
                        preferred_element_type=F32,
                    )
                    total = piece if total is None else total + piece
                if dy:
                    tsend[dy - 1, g, :, pl.ds(n * part, part)] = total.astype(BF16)
                else:
                    tsum[g, :, pl.ds(n * part, part)] = total
        if dy == 2:
            term_sent["a0"] = send(tsend.at[1, 0], trecv.at[0], y=yp)
            term_sent["a1"] = send(tsend.at[1, 1], trecv.at[1], y=ym)
        elif dy == 1:
            term_sent["d1"] = send(tsend.at[0, 1], trecv.at[2], y=yp)
        elif dy == 3:
            term_sent["d0"] = send(tsend.at[2, 0], trecv.at[3], y=ym)

    def terms_relay():
        term_sent["a0"].wait_recv()
        trecv[0] = (trecv[0].astype(F32) + tsend[0, 0].astype(F32)).astype(BF16)
        term_sent["b0"] = send(trecv.at[0], trecv.at[4], y=yp)
        term_sent["a1"].wait_recv()
        trecv[1] = (trecv[1].astype(F32) + tsend[2, 1].astype(F32)).astype(BF16)
        term_sent["b1"] = send(trecv.at[1], trecv.at[5], y=ym)

    def half_rows(which):
        return at(which * rows_yz, rows_yz, rows_yz)

    def terms_sum():
        term_sent["b0"].wait_recv()
        term_sent["d0"].wait_recv()
        term_sent["b1"].wait_recv()
        term_sent["d1"].wait_recv()
        for g, (i, j) in enumerate(((4, 3), (5, 2))):
            far = half_rows(1 - zl)
            tzs[g] = (tsum[g, far, :] + trecv[i, far, :].astype(F32) + trecv[j, far, :].astype(F32)).astype(BF16)
        term_sent["z"] = send(tzs, tzr, zl=1 - zl)

    def terms_back():
        term_sent["z"].wait_recv()
        for g, (i, j) in enumerate(((4, 3), (5, 2))):
            near = half_rows(zl)
            total = (
                tsum[g, near, :]
                + trecv[i, near, :].astype(F32)
                + trecv[j, near, :].astype(F32)
                + tzr[g].astype(F32)
            )
            for i in range(4):
                back[g * 4 + i] = total[i * tok : (i + 1) * tok, :].astype(BF16)
        for dc, dx in pairs:
            tx, tc = wrap(x + dx), lax.rem(c + dc, 2)
            term_sent[dc, dx] = send(back.at[tc * 4 + tx], ngf.at[mine], x=tx, c=tc)
        ngf[mine] = back[c * 4 + x]

    def norm_backward():
        for pair in pairs:
            term_sent[pair].wait_recv()
        grad = jnp.concatenate([ngf[i].astype(F32) for i in range(8)], axis=1)
        weighted = grad * gain_ref[...]
        scaled_now = scaled[...]
        first = jnp.mean(weighted, axis=-1, keepdims=True)
        second = jnp.mean(weighted * scaled_now, axis=-1, keepdims=True)
        result = stream_ref[...].astype(F32) + inverse[:, 0:1] * (weighted - first - scaled_now * second)
        dx_ref[...] = result.astype(BF16)

    stages = [
        lambda u: (product(u), rs_step(u, 0)),
        lambda u: rs_step(u, 1),
        lambda u: rs_step(u, 2),
        lambda u: rs_step(u, 3),
        lambda u: ag_step(u, 0),
        lambda u: ag_step(u, 1),
        lambda u: ag_step(u, 2),
        lambda u: ag_step(u, 3),
        finish,
    ]
    start = [0, 1, 2, 4, 6, 8]
    before = {
        0: [lambda: y_first(0), lambda: y_first(1), lambda: y_first(2), lambda: y_relay(0), lambda: y_relay(1)],
        1: [lambda: y_relay(2)],
        2: [q_forward],
        5: [w_forward],
        7: [q_last],
    }
    after = {
        8: [lambda: terms(2)],
        9: [lambda: terms(1), lambda: terms(3)],
        10: [terms_relay, lambda: terms(0)],
        12: [terms_sum],
        13: [terms_back],
        14: [norm_backward],
    }
    for tick in range(start[-1] + len(stages)):
        for action in before.get(tick, []):
            action()
        for u in range(len(units)):
            if 0 <= tick - start[u] < len(stages):
                stages[tick - start[u]](u)
        for action in after.get(tick, []):
            action()

    for copy in copies:
        copy.wait_send()
    for copy in locals_:
        if all(copy is not done for done in (q_local, w_local, own_in)):
            copy.wait()


N_COPIES = 140
N_LOCAL = 16


def shards(inputs, norm_gain, norm_bias, query_grad, stream_grad, query_weight):
    tok, width = inputs.shape
    rows, cols = query_grad.shape
    block = width // 8
    ordered = query_grad.reshape(4, 4, 2, tok, cols).transpose(1, 2, 0, 3, 4).reshape(rows, cols)
    vmem = pl.BlockSpec(memory_space=pltpu.VMEM)
    hbm = pl.BlockSpec(memory_space=pltpu.HBM)
    return pl.pallas_call(
        kernel,
        out_shape=(
            jax.ShapeDtypeStruct((tok, width), BF16),
            jax.ShapeDtypeStruct((width, cols), BF16),
        ),
        in_specs=[vmem, vmem, vmem, vmem, vmem, hbm],
        out_specs=(vmem, hbm),
        scratch_shapes=[
            pltpu.VMEM((tok, width), F32),
            pltpu.VMEM((tok, 128), F32),
            pltpu.VMEM((tok, width), BF16),
            pltpu.VMEM((8, tok, block), BF16),
            pltpu.VMEM((2, 4 * tok, block), BF16),
            pltpu.VMEM((2, rows, block), BF16),
            pltpu.VMEM((2, block, rows), BF16),
            pltpu.VMEM((4, 2, rows, cols), BF16),
            pltpu.VMEM((4, block, cols), BF16),
            pltpu.VMEM((2, block // 2, cols), BF16),
            pltpu.VMEM((4, block, cols), BF16),
            pltpu.VMEM((4, 2, 3, block // 8, cols), BF16),
            pltpu.VMEM((4, block // 4, cols), BF16),
            pltpu.VMEM((width, cols), BF16),
            pltpu.VMEM((3, 2, 8 * tok, block), BF16),
            pltpu.VMEM((6, 8 * tok, block), BF16),
            pltpu.VMEM((2, 8 * tok, block), F32),
            pltpu.VMEM((2, 4 * tok, block), BF16),
            pltpu.VMEM((2, 4 * tok, block), BF16),
            pltpu.VMEM((8, tok, block), BF16),
            pltpu.VMEM((8, tok, block), BF16),
            pltpu.SemaphoreType.DMA((N_COPIES,)),
            pltpu.SemaphoreType.DMA((N_COPIES,)),
            pltpu.SemaphoreType.DMA((N_LOCAL,)),
        ],
        compiler_params=pltpu.CompilerParams(
            collective_id=0, has_side_effects=True, vmem_limit_bytes=60 * 1024 * 1024
        ),
    )(inputs, norm_gain.reshape(1, width), norm_bias.reshape(1, width), ordered, stream_grad, query_weight)


def solution(mesh):
    torus = Mesh(mesh.devices.reshape(4, 2, 4, 4, 2), ALL)
    return jax.shard_map(
        shards,
        mesh=torus,
        in_specs=(P(ALL, None), P(), P(), P(DP, TENSOR), P(ALL, None), P(None, TENSOR)),
        out_specs=(P(ALL, None), P(None, TENSOR)),
        check_vma=False,
    )
```

time: 395 us -> 154 us (0.39)
  waiting for transfers between devices: 337 us -> 0 us
  Pallas kernels: 0 us -> 144 us
  matrix products: 19.8 us -> 0 us
  between operations: 15.3 us -> 0.64 us
  other arithmetic: 11.5 us -> 0 us
    pallas_call x0 -> x1, Pallas kernels: none -> 144 us  [shards(): pl.pallas_call(kernel, out_shape=(jax.ShapeDtypeStruct((tok, width), BF16...]
    all_gather x1 -> x0, waiting for transfers between devices: 124 us -> none  [shards(): lax.all_gather(inputs, TENSOR, axis=0, tiled=True)]
    psum x1 -> x0, waiting for transfers between devices: 110 us -> none  [shards(): lax.psum(lax.dot_general(piece_normed, grad_rows, (((0,), (0,)), ((), ())...]
    reduce_scatter x3 -> x0, waiting for transfers between devices: 103 us -> none  [sum_by_axis(): running = lax.psum_scatter(running, axis, scatter_dimension=0, tiled=True)]
    dot_general x2 -> x0, matrix products: 19.8 us -> none  [the longest x1 10 us: shards(): lax.dot_general(piece_normed, grad_rows, (((0,), (0,)), ((), ())), prefer...]
    reduce_sum x5 -> x0, other arithmetic: 9.54 us -> none  [the longest x2 5.44 us: normalize(): centre = jnp.mean(as_float, axis=-1, keepdims=True)]
  transfers between devices with their start and end apart: 5 -> 0, of which waited for: 4 -> 0; matrix products, arithmetic and copies ran while one was open for 6% -> 0% of each run, Pallas kernels for 0% -> 0%
where the time goes in v1:
time: 154 us
  Pallas kernels  144 us (94%)
  local copies, waits for them, and re-layouts  8.63 us (6%)
    pallas_call x1, Pallas kernels, shards(): pl.pallas_call(kernel, out_shape=(jax.ShapeDtypeStruct((tok, width), BF16...  144 us
    unnamed x2, local copies, waits for them, and re-layouts  6.69 us

profile of v1, /device:TPU:1, one launch (start us, length us, event | category | flops | bytes accessed | tf_op | source)
XLA Modules:
  0.0 153.7 jit_solution(1479554971539586744)
XLA Ops:
  0.6 1.9 %copy.8 = bf16[4,4,2,24,384]{4,3,0,2,1:T(8,128)(2,1)} copy(bf16[4,4,2,24,384]{4,3,2,1,0:T(8,128)(2,1)} %bitcast.7) | data formatting | bytes 1179648 | tf_op jit(solution)/shard_map/reshape | solution.py:390
  2.6 144.4 %shard_map.77 = (bf16[24,6144]{1,0:T(8,128)(2,1)}, bf16[6144,384]{1,0:T(8,128)(2,1)}) custom-call(bf16[24,6144]{1,0:T(8,128)(2,1)} %x_ref.1, f32[1,6144]{1,0:T(1,128)} %bitcast.8, f32[1,6144]{1,0:T(1,128)} %bitcast.9, bf16[768,384]{1,0:T(8,128)(2,1)} %bitcast.6, bf16[24,6144]{1,0:T(8,128)(2,1)} %stream_ref.1, bf16[6144,384]{1,0:T(8,128)(2,1)} %w_ref.1), custom_call_target="tpu_custom_call" | custom-call | tf_op jit(solution)/shard_map/pallas_call | solution.py:393
  147.0 1.7 %copy.11 = bf16[24,6144]{1,0:T(8,128)(2,1)} copy(bf16[24,6144]{1,0:T(8,128)(2,1)} %get-tuple-element.4) | data formatting | bytes 589824
  148.7 5.0 %copy.12 = bf16[6144,384]{1,0:T(8,128)(2,1)} copy(bf16[6144,384]{1,0:T(8,128)(2,1)} %get-tuple-element.5) | data formatting | bytes 9437184

commit v2 on v1

v2 whole, which is shorter than its diff:
```python
import jax
import jax.numpy as jnp
from jax import lax
from jax.experimental import pallas as pl
from jax.experimental.pallas import tpu as pltpu
from jax.sharding import Mesh
from jax.sharding import PartitionSpec as P

MESH = pl.DeviceIdType.MESH
DP = ("zh", "c")
TENSOR = ("x", "y", "zl")
ALL = DP + TENSOR
EPS = 1e-05

F32 = jnp.float32
BF16 = jnp.bfloat16


def kernel(
    x_ref, gain_ref, bias_ref, q_ref, stream_ref, w_ref, dx_ref, out,
    scaled, inverse, normed, spread, own, xs, xt, qs, ws, wrelay, gs, rsb, fin,
    tsend, trecv, tsum, tzs, tzr, back, ngf,
    send_sem, recv_sem, local_sem,
):
    zh, c, x, y, zl = [lax.axis_index(name) for name in ALL]
    tok, width = x_ref.shape
    block = width // 8
    cols = q_ref.shape[1]
    rows_yz = 4 * tok
    group = 8 * rows_yz
    sixth = block // 6
    bounds = [(0, sixth), (sixth, sixth), (2 * sixth, 2 * sixth), (4 * sixth, 2 * sixth)]
    sl = [pl.ds(*bound) for bound in bounds]

    def wrap(value):
        return lax.rem(value + 8, 4)

    xm, xp, xo = wrap(x - 1), wrap(x + 1), wrap(x + 2)
    ym, yp, yo = wrap(y - 1), wrap(y + 1), wrap(y + 2)
    zm, zp = wrap(zh - 1), wrap(zh + 1)
    other = 1 - c

    def at(offset, size, unit):
        return pl.ds(pl.multiple_of(offset, unit), size)

    copies = []
    locals_ = []

    def send(src, dst, **where):
        i = len(copies)
        copy = pltpu.make_async_remote_copy(
            src_ref=src,
            dst_ref=dst,
            send_sem=send_sem.at[i],
            recv_sem=recv_sem.at[i],
            device_id=where,
            device_id_type=MESH,
        )
        copy.start()
        copies.append(copy)
        return copy

    def local(src, dst):
        copy = pltpu.make_async_copy(src, dst, local_sem.at[len(locals_)])
        copy.start()
        locals_.append(copy)
        return copy

    pairs = [(dc, dx) for dc in range(2) for dx in range(4) if dc or dx]
    barrier = pltpu.get_barrier_semaphore()
    partners = [{"x": wrap(x + dx), "c": lax.rem(c + dc, 2)} for dc, dx in pairs]
    partners += [{"y": yp}, {"y": ym}, {"zl": 1 - zl}, {"zh": zp}, {"zh": zm}]
    for where in partners:
        pl.semaphore_signal(barrier, inc=1, device_id=where, device_id_type=MESH)

    mine = x * 2 + c
    w_local = local(w_ref.at[at(mine * block, block, block), :], ws.at[0])

    values = x_ref[...].astype(F32)
    centre = jnp.mean(values, axis=-1, keepdims=True)
    offsets = values - centre
    variance = jnp.mean(offsets * offsets, axis=-1, keepdims=True)
    inv = lax.rsqrt(variance + EPS)
    inverse[...] = jnp.broadcast_to(inv, inverse.shape)
    scaled[...] = offsets * inv
    normed[...] = (scaled[...] * gain_ref[...] + bias_ref[...]).astype(BF16)

    pl.semaphore_wait(barrier, len(partners))

    chunks = [(0, sixth), (sixth, 5 * sixth)]
    spread_in = []
    for begin, size in chunks:
        for dc, dx in pairs:
            tx, tc = wrap(x + dx), lax.rem(c + dc, 2)
            piece = normed.at[:, at((tx * 2 + tc) * block + begin, size, 128)]
            spread_in.append(send(piece, spread.at[c * 4 + x, :, pl.ds(begin, size)], x=tx, c=tc))

    for i in range(8):
        parts = [q_ref[(g * 8 + i) * tok : (g * 8 + i + 1) * tok, :].astype(F32) for g in range(4)]
        qs[0, c, i * rows_yz : (i + 1) * rows_yz, :] = jnp.concatenate(parts, axis=0).astype(BF16)
    q_d2d = {0: send(qs.at[0, c], qs.at[0, c], c=other)}
    q_down = send(qs.at[0, c], qs.at[1, c], x=xm)
    q_up = send(qs.at[0, c], qs.at[3, c], x=xp)

    spread[c * 4 + x] = normed[:, at(mine * block, block, 128)]
    base = y * 2 + zl
    own_in, zl_in = [], []
    for i, (begin, size) in enumerate(chunks):
        for copy in spread_in[i * len(pairs) : (i + 1) * len(pairs)]:
            copy.wait_recv()
        cut = pl.ds(begin, size)
        for g in range(2):
            parts = [spread[g * 4 + n, :, cut].astype(F32) for n in range(4)]
            own[g, :, cut] = jnp.concatenate(parts, axis=0).astype(BF16)
        own_in.append(local(own.at[:, :, cut], xs.at[:, at(base * rows_yz, rows_yz, rows_yz), cut]))
        for first, count in bounds:
            if begin <= first < begin + size:
                cut = pl.ds(first, count)
                zl_in.append(send(own.at[:, :, cut], xs.at[:, at(base * rows_yz, rows_yz, rows_yz), cut], zl=1 - zl))

    def w_rows(i, begin=0, size=block):
        return w_ref.at[at((i * 2 + c) * block + begin, size, size), :]

    w_down = send(w_rows(xm), ws.at[1], x=xm)
    w_up = send(w_rows(xp), ws.at[3], x=xp)
    half_w = block // 2

    y_up, y_down, relay_up, relay_down = {}, {}, {}, {}

    def y_rows(i):
        return at(i * 2 * rows_yz, 2 * rows_yz, 2 * rows_yz)

    def y_first(j):
        if j < 2:
            own_in[j].wait()
        zl_in[j].wait_recv()
        piece = xs.at[:, y_rows(y), sl[j]]
        y_up[j] = send(piece, piece, y=yp)
        y_down[j] = send(piece, piece, y=ym)

    def y_relay_up(j):
        y_up[j].wait_recv()
        piece = xs.at[0, y_rows(ym), sl[j]]
        relay_up[j] = send(piece, piece, y=yp)

    def y_relay_down(j):
        y_down[j].wait_recv()
        piece = xs.at[1, y_rows(yp), sl[j]]
        relay_down[j] = send(piece, piece, y=ym)

    units = [(k, first * sixth, size * sixth) for k, first, size in UNITS]

    def rows_of(u, q, h, base=0):
        _, begin, size = units[u]
        return at(base + begin + q * (size // 4) + h * (size // 8), size // 8, 16)

    ring = {}

    def prepare(j):
        begin, size = bounds[j]
        if not j:
            q_d2d[0].wait_recv()
        relay_up[j].wait_recv()
        relay_down[j].wait_recv()
        for g in range(2):
            xt[g, pl.ds(begin, size), :] = xs[g, :, pl.ds(begin, size)].T

    arrived = []

    def product(u):
        k, begin, size = units[u]
        if k and k not in arrived:
            arrived.append(k)
            q_d2d[k].wait_recv()
        piece = min(size, 2 * sixth)
        if size % piece:
            piece = sixth
        for first in range(begin, begin + size, piece):
            rows = pl.ds(first, piece)
            gs[k, rows, :] = (
                jnp.dot(xt[0, rows, :], qs[k, 0], preferred_element_type=F32)
                + jnp.dot(xt[1, rows, :], qs[k, 1], preferred_element_type=F32)
            ).astype(BF16)
        for d in range(2):
            ring[u, d, 0] = send(gs.at[k, rows_of(u, wrap(zh + (-1, 1)[d]), d), :], slot(u, d, 0), zh=(zp, zm)[d])

    def slot(u, d, s):
        k, begin, size = units[u]
        return rsb.at[k, d, s, pl.ds(begin // 8, size // 8), :]

    def source(k):
        return wrap(x - k) * 2 + c

    def rs_step(u, s, d):
        k, begin, size = units[u]
        ring[u, d, s - 1].wait_recv()
        sign = (-1, 1)[d]
        mine_part = gs[k, rows_of(u, wrap(zh + sign * (s + 1)), d), :].astype(F32)
        here = slot(u, d, s - 1)
        total = (here[...].astype(F32) + mine_part).astype(BF16)
        if s < 3:
            here[...] = total
            ring[u, d, s] = send(here, slot(u, d, s), zh=(zp, zm)[d])
        elif k == 0:
            out[rows_of(u, zh, d, mine * block), :] = total
        else:
            fin[k, pl.ds(begin // 4 + d * (size // 8), size // 8), :] = total

    def across(u):
        k, begin, size = units[u]
        landing = at(mine * block + begin + zh * (size // 4), size // 4, 32)
        ring[u, "x"] = send(fin.at[k, pl.ds(begin // 4, size // 4), :], out.at[landing, :], x=wrap(x + k))

    crossed = []

    def ag_step(u, s, d):
        k, begin, size = units[u]
        if s:
            ring[u, d, "a", s - 1].wait_recv()
        elif k and u not in crossed:
            crossed.append(u)
            ring[u, "x"].wait_recv()
        rows = out.at[rows_of(u, wrap(zh + (-1, 1)[d] * s), d, source(k) * block), :]
        ring[u, d, "a", s] = send(rows, rows, zh=(zp, zm)[d])

    def to_partner(u):
        k, begin, size = units[u]
        for d in range(2):
            ring[u, d, "a", 2].wait_recv()
        whole = at(source(k) * block + begin, size, 128)
        ring[u, "c"] = send(out.at[whole, :], out.at[whole, :], c=other)

    def finish(u):
        ring[u, "c"].wait_recv()

    q_relay, w_relay = {}, {}

    half = group // 2

    def q_forward_down():
        q_down.wait_recv()
        q_relay["down"] = send(qs.at[1, c, pl.ds(0, half), :], qs.at[2, c, pl.ds(0, half), :], x=xm)
        q_d2d[1] = send(qs.at[1, c], qs.at[1, c], c=other)

    def q_forward_up():
        q_up.wait_recv()
        q_relay["up"] = send(qs.at[3, c, pl.ds(half, half), :], qs.at[2, c, pl.ds(half, half), :], x=xp)
        q_d2d[3] = send(qs.at[3, c], qs.at[3, c], c=other)

    def w_first():
        w_relay["up"] = send(w_rows(xo, 0, half_w), wrelay.at[0], x=xp)
        w_relay["down"] = send(w_rows(xo, half_w, half_w), wrelay.at[1], x=xm)

    def q_last():
        q_relay["down"].wait_recv()
        q_relay["up"].wait_recv()
        q_d2d[2] = send(qs.at[2, c], qs.at[2, c], c=other)

    w_second = {}

    def w_forward_up():
        w_relay["up"].wait_recv()
        w_second["up"] = send(wrelay.at[0], ws.at[2, pl.ds(0, half_w), :], x=xp)

    def w_forward_down():
        w_relay["down"].wait_recv()
        w_second["down"] = send(wrelay.at[1], ws.at[2, pl.ds(half_w, half_w), :], x=xm)

    term_sent = {}

    def terms(dy):
        if dy == 2:
            w_local.wait()
            w_down.wait_recv()
            w_up.wait_recv()
            w_second["up"].wait_recv()
            w_second["down"].wait_recv()
        part = block // 3
        for g in range(2):
            for n in range(3):
                total = None
                for k in range(4):
                    piece = lax.dot_general(
                        qs[k, g, y_rows(wrap(y + dy)), :],
                        ws[k, pl.ds(n * part, part), :],
                        (((1,), (1,)), ((), ())),
                        preferred_element_type=F32,
                    )
                    total = piece if total is None else total + piece
                if dy:
                    tsend[dy - 1, g, :, pl.ds(n * part, part)] = total.astype(BF16)
                else:
                    tsum[g, :, pl.ds(n * part, part)] = total
        if dy == 2:
            term_sent["a0"] = send(tsend.at[1, 0], trecv.at[0], y=yp)
            term_sent["a1"] = send(tsend.at[1, 1], trecv.at[1], y=ym)
        elif dy == 1:
            term_sent["d1"] = send(tsend.at[0, 1], trecv.at[2], y=yp)
        elif dy == 3:
            term_sent["d0"] = send(tsend.at[2, 0], trecv.at[3], y=ym)

    def terms_relay_up():
        term_sent["a0"].wait_recv()
        trecv[0] = (trecv[0].astype(F32) + tsend[0, 0].astype(F32)).astype(BF16)
        term_sent["b0"] = send(trecv.at[0], trecv.at[4], y=yp)

    def terms_relay_down():
        term_sent["a1"].wait_recv()
        trecv[1] = (trecv[1].astype(F32) + tsend[2, 1].astype(F32)).astype(BF16)
        term_sent["b1"] = send(trecv.at[1], trecv.at[5], y=ym)

    def half_rows(which):
        return at(which * rows_yz, rows_yz, rows_yz)

    def terms_sum():
        term_sent["b0"].wait_recv()
        term_sent["d0"].wait_recv()
        term_sent["b1"].wait_recv()
        term_sent["d1"].wait_recv()
        for g, (i, j) in enumerate(((4, 3), (5, 2))):
            far = half_rows(1 - zl)
            tzs[g] = (tsum[g, far, :] + trecv[i, far, :].astype(F32) + trecv[j, far, :].astype(F32)).astype(BF16)
        term_sent["z"] = send(tzs, tzr, zl=1 - zl)

    def terms_back():
        term_sent["z"].wait_recv()
        for g, (i, j) in enumerate(((4, 3), (5, 2))):
            near = half_rows(zl)
            total = (
                tsum[g, near, :]
                + trecv[i, near, :].astype(F32)
                + trecv[j, near, :].astype(F32)
                + tzr[g].astype(F32)
            )
            for i in range(4):
                back[g * 4 + i] = total[i * tok : (i + 1) * tok, :].astype(BF16)
        for dc, dx in pairs:
            tx, tc = wrap(x + dx), lax.rem(c + dc, 2)
            term_sent[dc, dx] = send(back.at[tc * 4 + tx], ngf.at[mine], x=tx, c=tc)
        ngf[mine] = back[c * 4 + x]

    def norm_backward():
        for pair in pairs:
            term_sent[pair].wait_recv()
        grad = jnp.concatenate([ngf[i].astype(F32) for i in range(8)], axis=1)
        weighted = grad * gain_ref[...]
        scaled_now = scaled[...]
        first = jnp.mean(weighted, axis=-1, keepdims=True)
        second = jnp.mean(weighted * scaled_now, axis=-1, keepdims=True)
        result = stream_ref[...].astype(F32) + inverse[:, 0:1] * (weighted - first - scaled_now * second)
        dx_ref[...] = result.astype(BF16)

    actions = {
        "yf": y_first, "yu": y_relay_up, "yd": y_relay_down, "prep": prepare, "P": product, "R": rs_step,
        "X": across, "A": ag_step, "D": to_partner, "F": finish, "qd": q_forward_down, "qu": q_forward_up,
        "ql": q_last, "wr": w_first, "wfu": w_forward_up, "wfd": w_forward_down, "T": terms,
        "tr0": terms_relay_up, "tr1": terms_relay_down, "ts": terms_sum, "tb": terms_back, "nb": norm_backward,
    }
    for name, *rest in ORDER:
        actions[name](*rest)

    for copy in copies:
        copy.wait_send()


N_COPIES = 224
N_LOCAL = 8

ORDER = [
    ("yf", 0), ("yf", 1), ("yf", 2), ("yu", 0), ("yd", 0), ("yf", 3), ("yu", 1), ("yd", 1), ("qd",), ("qu",),
    ("wr",), ("yu", 2), ("yd", 2), ("prep", 0), ("P", 0), ("R", 0, 1, 0), ("yu", 3), ("yd", 3), ("R", 0, 1, 1),
    ("prep", 1), ("P", 1), ("P", 2), ("P", 3), ("prep", 2), ("P", 4), ("R", 0, 2, 0), ("R", 0, 2, 1), ("R", 1, 1, 0),
    ("prep", 3), ("P", 5), ("P", 6), ("P", 7), ("R", 1, 1, 1), ("R", 2, 1, 0), ("R", 2, 1, 1), ("R", 3, 1, 0),
    ("R", 3, 1, 1), ("R", 4, 1, 0), ("R", 4, 1, 1), ("R", 1, 2, 0), ("R", 0, 3, 0), ("R", 0, 3, 1), ("R", 5, 1, 0),
    ("R", 5, 1, 1), ("A", 0, 0, 0), ("A", 0, 0, 1), ("ql",), ("R", 6, 1, 0), ("R", 6, 1, 1), ("P", 8), ("P", 9),
    ("R", 7, 1, 0), ("R", 7, 1, 1), ("R", 1, 2, 1), ("R", 2, 2, 0), ("R", 2, 2, 1), ("R", 3, 2, 0), ("R", 3, 2, 1),
    ("R", 4, 2, 0), ("wfu",), ("wfd",), ("R", 4, 2, 1), ("R", 1, 3, 0), ("R", 5, 2, 0), ("R", 5, 2, 1),
    ("A", 0, 1, 0), ("A", 0, 1, 1), ("R", 6, 2, 0), ("R", 6, 2, 1), ("R", 8, 1, 0), ("R", 8, 1, 1), ("R", 9, 1, 0),
    ("R", 9, 1, 1), ("T", 2), ("T", 1), ("T", 3), ("T", 0), ("R", 7, 2, 0), ("R", 7, 2, 1), ("R", 1, 3, 1),
    ("R", 2, 3, 0), ("R", 2, 3, 1), ("X", 2), ("R", 3, 3, 0), ("R", 3, 3, 1), ("X", 3), ("R", 4, 3, 0),
    ("R", 4, 3, 1), ("R", 5, 3, 0), ("R", 5, 3, 1), ("R", 6, 3, 0), ("R", 6, 3, 1), ("R", 8, 2, 0), ("X", 6),
    ("A", 1, 0, 0), ("A", 1, 0, 1), ("A", 4, 0, 0), ("R", 8, 2, 1), ("tr0",), ("tr1",), ("A", 4, 0, 1),
    ("A", 5, 0, 0), ("A", 5, 0, 1), ("A", 0, 2, 0), ("A", 0, 2, 1), ("R", 9, 2, 0), ("A", 2, 0, 0), ("A", 2, 0, 1),
    ("A", 3, 0, 0), ("R", 9, 2, 1), ("A", 3, 0, 1), ("R", 7, 3, 0), ("R", 7, 3, 1), ("X", 7), ("A", 6, 0, 0),
    ("A", 6, 0, 1), ("A", 1, 1, 1), ("R", 8, 3, 0), ("A", 1, 1, 0), ("R", 8, 3, 1), ("X", 8), ("A", 4, 1, 0),
    ("A", 4, 1, 1), ("A", 5, 1, 0), ("A", 5, 1, 1), ("A", 7, 0, 0), ("A", 7, 0, 1), ("D", 0), ("R", 9, 3, 0),
    ("A", 2, 1, 1), ("F", 0), ("A", 8, 0, 0), ("A", 8, 0, 1), ("A", 2, 1, 0), ("R", 9, 3, 1), ("X", 9),
    ("A", 3, 1, 0), ("A", 3, 1, 1), ("ts",), ("A", 6, 1, 0), ("A", 6, 1, 1), ("A", 1, 2, 0), ("A", 1, 2, 1),
    ("A", 4, 2, 0), ("A", 9, 0, 0), ("A", 9, 0, 1), ("A", 4, 2, 1), ("A", 5, 2, 0), ("A", 5, 2, 1), ("A", 7, 1, 0),
    ("A", 7, 1, 1), ("A", 8, 1, 0), ("A", 2, 2, 1), ("A", 2, 2, 0), ("A", 8, 1, 1), ("A", 3, 2, 0), ("A", 3, 2, 1),
    ("A", 6, 2, 1), ("A", 9, 1, 1), ("tb",), ("A", 6, 2, 0), ("A", 7, 2, 1), ("D", 1), ("D", 4), ("F", 1), ("F", 4),
    ("A", 9, 1, 0), ("A", 8, 2, 1), ("nb",), ("D", 5), ("F", 5), ("A", 7, 2, 0), ("A", 8, 2, 0), ("A", 9, 2, 1),
    ("D", 2), ("D", 3), ("F", 2), ("F", 3), ("D", 6), ("A", 9, 2, 0), ("F", 6), ("D", 7), ("D", 8), ("F", 7),
    ("F", 8), ("D", 9), ("F", 9),
]
UNITS = [(0, 0, 1), (0, 1, 1), (1, 0, 2), (3, 0, 2), (0, 2, 2), (0, 4, 2), (1, 2, 4), (3, 2, 4), (2, 0, 3), (2, 3, 3)]


def shards(inputs, norm_gain, norm_bias, query_grad, stream_grad, query_weight):
    tok, width = inputs.shape
    rows, cols = query_grad.shape
    block = width // 8
    vmem = pl.BlockSpec(memory_space=pltpu.VMEM)
    hbm = pl.BlockSpec(memory_space=pltpu.HBM)
    return pl.pallas_call(
        kernel,
        out_shape=(
            jax.ShapeDtypeStruct((tok, width), BF16),
            jax.ShapeDtypeStruct((width, cols), BF16),
        ),
        in_specs=[vmem, vmem, vmem, vmem, vmem, hbm],
        out_specs=(vmem, vmem),
        scratch_shapes=[
            pltpu.VMEM((tok, width), F32),
            pltpu.VMEM((tok, 128), F32),
            pltpu.VMEM((tok, width), BF16),
            pltpu.VMEM((8, tok, block), BF16),
            pltpu.VMEM((2, 4 * tok, block), BF16),
            pltpu.VMEM((2, rows, block), BF16),
            pltpu.VMEM((2, block, rows), BF16),
            pltpu.VMEM((4, 2, rows, cols), BF16),
            pltpu.VMEM((4, block, cols), BF16),
            pltpu.VMEM((2, block // 2, cols), BF16),
            pltpu.VMEM((4, block, cols), BF16),
            pltpu.VMEM((4, 2, 3, block // 8, cols), BF16),
            pltpu.VMEM((4, block // 4, cols), BF16),
            pltpu.VMEM((3, 2, 8 * tok, block), BF16),
            pltpu.VMEM((6, 8 * tok, block), BF16),
            pltpu.VMEM((2, 8 * tok, block), F32),
            pltpu.VMEM((2, 4 * tok, block), BF16),
            pltpu.VMEM((2, 4 * tok, block), BF16),
            pltpu.VMEM((8, tok, block), BF16),
            pltpu.VMEM((8, tok, block), BF16),
            pltpu.SemaphoreType.DMA((N_COPIES,)),
            pltpu.SemaphoreType.DMA((N_COPIES,)),
            pltpu.SemaphoreType.DMA((N_LOCAL,)),
        ],
        compiler_params=pltpu.CompilerParams(
            collective_id=0, has_side_effects=True, vmem_limit_bytes=44 * 1024 * 1024
        ),
    )(inputs, norm_gain.reshape(1, width), norm_bias.reshape(1, width), query_grad, stream_grad, query_weight)


def solution(mesh):
    torus = Mesh(mesh.devices.reshape(4, 2, 4, 4, 2), ALL)
    return jax.shard_map(
        shards,
        mesh=torus,
        in_specs=(P(ALL, None), P(), P(), P(DP, TENSOR), P(ALL, None), P(None, TENSOR)),
        out_specs=(P(ALL, None), P(None, TENSOR)),
        check_vma=False,
    )
```

time: 154 us -> 135 us (0.88)
  Pallas kernels: 144 us -> 126 us
    pallas_call x1, Pallas kernels: 144 us -> 126 us  [shards(): pl.pallas_call(kernel, out_shape=(jax.ShapeDtypeStruct((tok, width), BF16...]
    reshape x1 -> x0, local copies, waits for them, and re-layouts: 1.94 us -> none  [shards(): query_grad.reshape(4, 4, 2, tok, cols).transpose(1, 2, 0, 3, 4)]
    unnamed x2 -> x12, local copies, waits for them, and re-layouts: 6.69 us -> 7.35 us
where the time goes in v2:
time: 135 us; the launch traced here: 134 us
  Pallas kernels  126 us (93%)
  local copies, waits for them, and re-layouts  7.35 us (5%)
    pallas_call x1, Pallas kernels, shards(): pl.pallas_call(kernel, out_shape=(jax.ShapeDtypeStruct((tok, width), BF16...  126 us
    unnamed x12, local copies, waits for them, and re-layouts  7.35 us

profile of v2, /device:TPU:1, one launch (start us, length us, event | category | flops | bytes accessed | tf_op | source)
XLA Modules:
  0.0 133.8 jit_solution(13560104387435140292)
XLA Ops:
  0.6 0.0 copy-start
  0.6 1.1 copy-done
  1.7 0.0 copy-start.1
  1.7 1.0 copy-done.1
  2.7 0.0 copy-start.2
  2.7 1.0 copy-done.2
  3.6 0.0 copy-start.3
  3.6 0.7 copy-done.3
  4.4 0.0 copy-start.4
  4.4 0.7 copy-done.4
  5.1 125.8 %shard_map.77 = (bf16[24,6144]{1,0:T(8,128)(2,1)S(1)}, bf16[6144,384]{1,0:T(8,128)(2,1)S(1)}) custom-call(bf16[24,6144]{1,0:T(8,128)(2,1)S(1)} %copy-done.1, f32[1,6144]{1,0:T(1,128)S(1)} %bitcast.2, f32[1,6144]{1,0:T(1,128)S(1)} %bitcast.3, bf16[768,384]{1,0:T(8,128)(2,1)S(1)} %copy-done, bf16[24,6144]{1,0:T(8,128)(2,1)S(1)} %copy-done.2, ...), custom_call_target="tpu_custom_call" | custom-call | tf_op jit(solution)/shard_map/pallas_call | solution.py:405
  130.9 0.7 copy.10
  131.6 2.2 %copy.11 = bf16[6144,384]{1,0:T(8,128)(2,1)} copy(bf16[6144,384]{1,0:T(8,128)(2,1)S(1)} %get-tuple-element.5) | data formatting | bytes 9437184
Async XLA Ops:
  0.6 1.1 copy-start
  1.7 1.0 copy-start.1
  2.7 1.0 copy-start.2
  3.6 0.7 copy-start.3
  4.4 0.7 copy-start.4

commit v3 on v2

--- a/solution.py
+++ b/solution.py
@@ -17,7 +17,8 @@
 
 
 def kernel(
-    x_ref, gain_ref, bias_ref, q_ref, stream_ref, w_ref, dx_ref, out,
+    x_hbm, gain_hbm, bias_hbm, q_hbm, stream_hbm, w_ref, dx_ref, out,
+    x_ref, gain_ref, bias_ref, q_ref, stream_ref,
     scaled, inverse, normed, spread, own, xs, xt, qs, ws, wrelay, gs, rsb, fin,
     tsend, trecv, tsum, tzs, tzr, back, ngf,
     send_sem, recv_sem, local_sem,
@@ -29,7 +30,7 @@
     rows_yz = 4 * tok
     group = 8 * rows_yz
     sixth = block // 6
-    bounds = [(0, sixth), (sixth, sixth), (2 * sixth, 2 * sixth), (4 * sixth, 2 * sixth)]
+    bounds = [(i * sixth, sixth) for i in range(6)]
     sl = [pl.ds(*bound) for bound in bounds]
 
     def wrap(value):
@@ -66,6 +67,8 @@
         locals_.append(copy)
         return copy
 
+    first_loads = [local(x_hbm, x_ref), local(gain_hbm, gain_ref), local(bias_hbm, bias_ref)]
+
     pairs = [(dc, dx) for dc in range(2) for dx in range(4) if dc or dx]
     barrier = pltpu.get_barrier_semaphore()
     partners = [{"x": wrap(x + dx), "c": lax.rem(c + dc, 2)} for dc, dx in pairs]
@@ -74,8 +77,12 @@
         pl.semaphore_signal(barrier, inc=1, device_id=where, device_id_type=MESH)
 
     mine = x * 2 + c
+    q_local = local(q_hbm, q_ref)
+    stream_local = local(stream_hbm, stream_ref)
     w_local = local(w_ref.at[at(mine * block, block, block), :], ws.at[0])
 
+    for copy in first_loads:
+        copy.wait()
     values = x_ref[...].astype(F32)
     centre = jnp.mean(values, axis=-1, keepdims=True)
     offsets = values - centre
@@ -95,6 +102,7 @@
             piece = normed.at[:, at((tx * 2 + tc) * block + begin, size, 128)]
             spread_in.append(send(piece, spread.at[c * 4 + x, :, pl.ds(begin, size)], x=tx, c=tc))
 
+    q_local.wait()
     for i in range(8):
         parts = [q_ref[(g * 8 + i) * tok : (g * 8 + i + 1) * tok, :].astype(F32) for g in range(4)]
         qs[0, c, i * rows_yz : (i + 1) * rows_yz, :] = jnp.concatenate(parts, axis=0).astype(BF16)
@@ -347,6 +355,7 @@
         scaled_now = scaled[...]
         first = jnp.mean(weighted, axis=-1, keepdims=True)
         second = jnp.mean(weighted * scaled_now, axis=-1, keepdims=True)
+        stream_local.wait()
         result = stream_ref[...].astype(F32) + inverse[:, 0:1] * (weighted - first - scaled_now * second)
         dx_ref[...] = result.astype(BF16)
 
@@ -367,31 +376,32 @@
 N_LOCAL = 8
 
 ORDER = [
-    ("yf", 0), ("yf", 1), ("yf", 2), ("yu", 0), ("yd", 0), ("yf", 3), ("yu", 1), ("yd", 1), ("qd",), ("qu",),
-    ("wr",), ("yu", 2), ("yd", 2), ("prep", 0), ("P", 0), ("R", 0, 1, 0), ("yu", 3), ("yd", 3), ("R", 0, 1, 1),
-    ("prep", 1), ("P", 1), ("P", 2), ("P", 3), ("prep", 2), ("P", 4), ("R", 0, 2, 0), ("R", 0, 2, 1), ("R", 1, 1, 0),
-    ("prep", 3), ("P", 5), ("P", 6), ("P", 7), ("R", 1, 1, 1), ("R", 2, 1, 0), ("R", 2, 1, 1), ("R", 3, 1, 0),
-    ("R", 3, 1, 1), ("R", 4, 1, 0), ("R", 4, 1, 1), ("R", 1, 2, 0), ("R", 0, 3, 0), ("R", 0, 3, 1), ("R", 5, 1, 0),
-    ("R", 5, 1, 1), ("A", 0, 0, 0), ("A", 0, 0, 1), ("ql",), ("R", 6, 1, 0), ("R", 6, 1, 1), ("P", 8), ("P", 9),
-    ("R", 7, 1, 0), ("R", 7, 1, 1), ("R", 1, 2, 1), ("R", 2, 2, 0), ("R", 2, 2, 1), ("R", 3, 2, 0), ("R", 3, 2, 1),
-    ("R", 4, 2, 0), ("wfu",), ("wfd",), ("R", 4, 2, 1), ("R", 1, 3, 0), ("R", 5, 2, 0), ("R", 5, 2, 1),
-    ("A", 0, 1, 0), ("A", 0, 1, 1), ("R", 6, 2, 0), ("R", 6, 2, 1), ("R", 8, 1, 0), ("R", 8, 1, 1), ("R", 9, 1, 0),
-    ("R", 9, 1, 1), ("T", 2), ("T", 1), ("T", 3), ("T", 0), ("R", 7, 2, 0), ("R", 7, 2, 1), ("R", 1, 3, 1),
-    ("R", 2, 3, 0), ("R", 2, 3, 1), ("X", 2), ("R", 3, 3, 0), ("R", 3, 3, 1), ("X", 3), ("R", 4, 3, 0),
-    ("R", 4, 3, 1), ("R", 5, 3, 0), ("R", 5, 3, 1), ("R", 6, 3, 0), ("R", 6, 3, 1), ("R", 8, 2, 0), ("X", 6),
-    ("A", 1, 0, 0), ("A", 1, 0, 1), ("A", 4, 0, 0), ("R", 8, 2, 1), ("tr0",), ("tr1",), ("A", 4, 0, 1),
-    ("A", 5, 0, 0), ("A", 5, 0, 1), ("A", 0, 2, 0), ("A", 0, 2, 1), ("R", 9, 2, 0), ("A", 2, 0, 0), ("A", 2, 0, 1),
-    ("A", 3, 0, 0), ("R", 9, 2, 1), ("A", 3, 0, 1), ("R", 7, 3, 0), ("R", 7, 3, 1), ("X", 7), ("A", 6, 0, 0),
-    ("A", 6, 0, 1), ("A", 1, 1, 1), ("R", 8, 3, 0), ("A", 1, 1, 0), ("R", 8, 3, 1), ("X", 8), ("A", 4, 1, 0),
-    ("A", 4, 1, 1), ("A", 5, 1, 0), ("A", 5, 1, 1), ("A", 7, 0, 0), ("A", 7, 0, 1), ("D", 0), ("R", 9, 3, 0),
-    ("A", 2, 1, 1), ("F", 0), ("A", 8, 0, 0), ("A", 8, 0, 1), ("A", 2, 1, 0), ("R", 9, 3, 1), ("X", 9),
-    ("A", 3, 1, 0), ("A", 3, 1, 1), ("ts",), ("A", 6, 1, 0), ("A", 6, 1, 1), ("A", 1, 2, 0), ("A", 1, 2, 1),
-    ("A", 4, 2, 0), ("A", 9, 0, 0), ("A", 9, 0, 1), ("A", 4, 2, 1), ("A", 5, 2, 0), ("A", 5, 2, 1), ("A", 7, 1, 0),
-    ("A", 7, 1, 1), ("A", 8, 1, 0), ("A", 2, 2, 1), ("A", 2, 2, 0), ("A", 8, 1, 1), ("A", 3, 2, 0), ("A", 3, 2, 1),
-    ("A", 6, 2, 1), ("A", 9, 1, 1), ("tb",), ("A", 6, 2, 0), ("A", 7, 2, 1), ("D", 1), ("D", 4), ("F", 1), ("F", 4),
-    ("A", 9, 1, 0), ("A", 8, 2, 1), ("nb",), ("D", 5), ("F", 5), ("A", 7, 2, 0), ("A", 8, 2, 0), ("A", 9, 2, 1),
-    ("D", 2), ("D", 3), ("F", 2), ("F", 3), ("D", 6), ("A", 9, 2, 0), ("F", 6), ("D", 7), ("D", 8), ("F", 7),
-    ("F", 8), ("D", 9), ("F", 9),
+    ("yf", 0), ("yf", 1), ("yu", 0), ("yd", 0), ("yf", 2), ("yu", 1), ("yd", 1), ("yf", 3), ("prep", 0), ("P", 0),
+    ("qd",), ("yu", 2), ("yd", 2), ("yf", 4), ("prep", 1), ("qu",), ("wr",), ("P", 1), ("P", 2), ("R", 0, 1, 0),
+    ("R", 0, 1, 1), ("yu", 3), ("yd", 3), ("yf", 5), ("P", 3), ("prep", 2), ("R", 1, 1, 0), ("R", 1, 1, 1),
+    ("yu", 4), ("yd", 4), ("R", 2, 1, 0), ("R", 2, 1, 1), ("R", 0, 2, 0), ("R", 0, 2, 1), ("prep", 3), ("P", 4),
+    ("R", 3, 1, 0), ("R", 3, 1, 1), ("R", 1, 2, 0), ("R", 1, 2, 1), ("yu", 5), ("yd", 5), ("prep", 4),
+    ("R", 2, 2, 0), ("R", 2, 2, 1), ("R", 0, 3, 0), ("R", 0, 3, 1), ("A", 0, 0, 0), ("A", 0, 0, 1), ("R", 4, 1, 0),
+    ("R", 4, 1, 1), ("prep", 5), ("P", 5), ("P", 6), ("P", 7), ("R", 3, 2, 0), ("R", 3, 2, 1), ("R", 1, 3, 0),
+    ("R", 1, 3, 1), ("R", 4, 2, 0), ("R", 4, 2, 1), ("R", 2, 3, 0), ("R", 2, 3, 1), ("X", 2), ("A", 1, 0, 0),
+    ("A", 1, 0, 1), ("A", 0, 1, 0), ("A", 0, 1, 1), ("R", 5, 1, 0), ("R", 5, 1, 1), ("R", 6, 1, 0), ("R", 6, 1, 1),
+    ("ql",), ("R", 7, 1, 0), ("R", 7, 1, 1), ("P", 8), ("P", 9), ("R", 3, 3, 0), ("R", 3, 3, 1), ("X", 3),
+    ("R", 4, 3, 0), ("R", 4, 3, 1), ("A", 4, 0, 0), ("A", 4, 0, 1), ("A", 1, 1, 0), ("A", 1, 1, 1), ("A", 0, 2, 0),
+    ("wfd",), ("A", 0, 2, 1), ("R", 5, 2, 0), ("R", 5, 2, 1), ("wfu",), ("A", 3, 0, 0), ("A", 3, 0, 1),
+    ("A", 2, 0, 0), ("A", 2, 0, 1), ("R", 6, 2, 0), ("R", 6, 2, 1), ("R", 7, 2, 0), ("R", 7, 2, 1), ("R", 8, 1, 0),
+    ("R", 8, 1, 1), ("R", 9, 1, 0), ("R", 9, 1, 1), ("A", 4, 1, 0), ("A", 4, 1, 1), ("A", 1, 2, 0), ("T", 2),
+    ("T", 1), ("T", 3), ("T", 0), ("R", 5, 3, 0), ("R", 5, 3, 1), ("R", 6, 3, 0), ("R", 6, 3, 1), ("X", 6),
+    ("R", 7, 3, 0), ("R", 7, 3, 1), ("X", 7), ("A", 5, 0, 0), ("A", 5, 0, 1), ("A", 2, 1, 0), ("A", 2, 1, 1),
+    ("A", 3, 1, 0), ("A", 3, 1, 1), ("A", 1, 2, 1), ("D", 0), ("R", 8, 2, 0), ("R", 8, 2, 1), ("F", 0), ("tr0",),
+    ("tr1",), ("R", 9, 2, 0), ("R", 9, 2, 1), ("A", 4, 2, 0), ("A", 4, 2, 1), ("A", 6, 0, 0), ("A", 6, 0, 1),
+    ("A", 7, 0, 0), ("A", 7, 0, 1), ("A", 5, 1, 1), ("A", 5, 1, 0), ("A", 2, 2, 1), ("A", 2, 2, 0), ("A", 3, 2, 1),
+    ("A", 3, 2, 0), ("D", 1), ("F", 1), ("R", 8, 3, 0), ("R", 8, 3, 1), ("X", 8), ("R", 9, 3, 0), ("R", 9, 3, 1),
+    ("X", 9), ("D", 4), ("F", 4), ("A", 6, 1, 0), ("A", 6, 1, 1), ("A", 8, 0, 0), ("A", 8, 0, 1), ("ts",),
+    ("A", 9, 0, 0), ("A", 9, 0, 1), ("A", 7, 1, 0), ("A", 7, 1, 1), ("A", 5, 2, 0), ("A", 5, 2, 1), ("D", 2),
+    ("D", 3), ("F", 2), ("F", 3), ("A", 6, 2, 0), ("A", 6, 2, 1), ("A", 8, 1, 0), ("A", 8, 1, 1), ("tb",),
+    ("A", 9, 1, 0), ("A", 9, 1, 1), ("A", 7, 2, 0), ("A", 7, 2, 1), ("D", 5), ("nb",), ("F", 5), ("D", 6),
+    ("A", 8, 2, 0), ("A", 8, 2, 1), ("F", 6), ("A", 9, 2, 0), ("A", 9, 2, 1), ("D", 7), ("D", 8), ("F", 7), ("F", 8),
+    ("D", 9), ("F", 9),
 ]
 UNITS = [(0, 0, 1), (0, 1, 1), (1, 0, 2), (3, 0, 2), (0, 2, 2), (0, 4, 2), (1, 2, 4), (3, 2, 4), (2, 0, 3), (2, 3, 3)]
 
@@ -405,12 +415,17 @@
     return pl.pallas_call(
         kernel,
         out_shape=(
-            jax.ShapeDtypeStruct((tok, width), BF16),
-            jax.ShapeDtypeStruct((width, cols), BF16),
+            pltpu.VMEM((tok, width), BF16),
+            pltpu.VMEM((width, cols), BF16),
         ),
-        in_specs=[vmem, vmem, vmem, vmem, vmem, hbm],
+        in_specs=[hbm] * 6,
         out_specs=(vmem, vmem),
         scratch_shapes=[
+            pltpu.VMEM((tok, width), BF16),
+            pltpu.VMEM((1, width), F32),
+            pltpu.VMEM((1, width), F32),
+            pltpu.VMEM((rows, cols), BF16),
+            pltpu.VMEM((tok, width), BF16),
             pltpu.VMEM((tok, width), F32),
             pltpu.VMEM((tok, 128), F32),
             pltpu.VMEM((tok, width), BF16),
@@ -436,7 +451,7 @@
             pltpu.SemaphoreType.DMA((N_LOCAL,)),
         ],
         compiler_params=pltpu.CompilerParams(
-            collective_id=0, has_side_effects=True, vmem_limit_bytes=44 * 1024 * 1024
+            collective_id=0, has_side_effects=True, vmem_limit_bytes=57 * 1024 * 1024
         ),
     )(inputs, norm_gain.reshape(1, width), norm_bias.reshape(1, width), query_grad, stream_grad, query_weight)
 

time: 135 us -> 126 us (0.933); the launches traced: 134 us -> 126 us
  local copies, waits for them, and re-layouts: 7.35 us -> 2.9 us
  Pallas kernels: 126 us -> 123 us
    unnamed x12 -> x2, local copies, waits for them, and re-layouts: 7.35 us -> 2.9 us
    pallas_call x1, Pallas kernels: 126 us -> 123 us  [shards(): pl.pallas_call(kernel, out_shape=(pltpu.VMEM((tok, width), BF16), pltpu.V...]
where the time goes in v3:
time: 126 us
  Pallas kernels  123 us (98%)
  local copies, waits for them, and re-layouts  2.9 us (2%)
    pallas_call x1, Pallas kernels, shards(): pl.pallas_call(kernel, out_shape=(pltpu.VMEM((tok, width), BF16), pltpu.V...  123 us
    unnamed x2, local copies, waits for them, and re-layouts  2.9 us

profile of v3, /device:TPU:1, one launch (start us, length us, event | category | flops | bytes accessed | tf_op | source)
XLA Modules:
  0.0 126.2 jit_solution(10469391118277092210)
XLA Ops:
  0.6 122.6 %shard_map.77 = (bf16[24,6144]{1,0:T(8,128)(2,1)S(1)}, bf16[6144,384]{1,0:T(8,128)(2,1)S(1)}) custom-call(bf16[24,6144]{1,0:T(8,128)(2,1)} %x_hbm.1, f32[1,6144]{1,0:T(1,128)} %bitcast.2, f32[1,6144]{1,0:T(1,128)} %bitcast.3, bf16[768,384]{1,0:T(8,128)(2,1)} %q_hbm.1, bf16[24,6144]{1,0:T(8,128)(2,1)} %stream_hbm.1, bf16[6144,384]{1,0:T(8,128)(2,1)} %w_ref.1), custom_call_target="tpu_custom_call" | custom-call | tf_op jit(solution)/shard_map/pallas_call | solution.py:415
  123.3 0.7 copy.10
  124.0 2.2 %copy.11 = bf16[6144,384]{1,0:T(8,128)(2,1)} copy(bf16[6144,384]{1,0:T(8,128)(2,1)S(1)} %get-tuple-element.3) | data formatting | bytes 9437184

commit v4 on v3

--- a/solution.py
+++ b/solution.py
@@ -276,13 +276,20 @@
 
     term_sent = {}
 
+    waited = []
+
     def terms(dy):
-        if dy == 2:
+        if not waited:
+            waited.append(True)
             w_local.wait()
             w_down.wait_recv()
             w_up.wait_recv()
             w_second["up"].wait_recv()
             w_second["down"].wait_recv()
+            for k in (1, 2, 3):
+                if k not in arrived:
+                    arrived.append(k)
+                    q_d2d[k].wait_recv()
         part = block // 3
         for g in range(2):
             for n in range(3):
@@ -372,38 +379,54 @@
         copy.wait_send()
 
 
-N_COPIES = 224
+N_COPIES = 256
 N_LOCAL = 8
 
 ORDER = [
     ("yf", 0), ("yf", 1), ("yu", 0), ("yd", 0), ("yf", 2), ("yu", 1), ("yd", 1), ("yf", 3), ("prep", 0), ("P", 0),
-    ("qd",), ("yu", 2), ("yd", 2), ("yf", 4), ("prep", 1), ("qu",), ("wr",), ("P", 1), ("P", 2), ("R", 0, 1, 0),
-    ("R", 0, 1, 1), ("yu", 3), ("yd", 3), ("yf", 5), ("P", 3), ("prep", 2), ("R", 1, 1, 0), ("R", 1, 1, 1),
-    ("yu", 4), ("yd", 4), ("R", 2, 1, 0), ("R", 2, 1, 1), ("R", 0, 2, 0), ("R", 0, 2, 1), ("prep", 3), ("P", 4),
-    ("R", 3, 1, 0), ("R", 3, 1, 1), ("R", 1, 2, 0), ("R", 1, 2, 1), ("yu", 5), ("yd", 5), ("prep", 4),
-    ("R", 2, 2, 0), ("R", 2, 2, 1), ("R", 0, 3, 0), ("R", 0, 3, 1), ("A", 0, 0, 0), ("A", 0, 0, 1), ("R", 4, 1, 0),
-    ("R", 4, 1, 1), ("prep", 5), ("P", 5), ("P", 6), ("P", 7), ("R", 3, 2, 0), ("R", 3, 2, 1), ("R", 1, 3, 0),
-    ("R", 1, 3, 1), ("R", 4, 2, 0), ("R", 4, 2, 1), ("R", 2, 3, 0), ("R", 2, 3, 1), ("X", 2), ("A", 1, 0, 0),
-    ("A", 1, 0, 1), ("A", 0, 1, 0), ("A", 0, 1, 1), ("R", 5, 1, 0), ("R", 5, 1, 1), ("R", 6, 1, 0), ("R", 6, 1, 1),
-    ("ql",), ("R", 7, 1, 0), ("R", 7, 1, 1), ("P", 8), ("P", 9), ("R", 3, 3, 0), ("R", 3, 3, 1), ("X", 3),
-    ("R", 4, 3, 0), ("R", 4, 3, 1), ("A", 4, 0, 0), ("A", 4, 0, 1), ("A", 1, 1, 0), ("A", 1, 1, 1), ("A", 0, 2, 0),
-    ("wfd",), ("A", 0, 2, 1), ("R", 5, 2, 0), ("R", 5, 2, 1), ("wfu",), ("A", 3, 0, 0), ("A", 3, 0, 1),
-    ("A", 2, 0, 0), ("A", 2, 0, 1), ("R", 6, 2, 0), ("R", 6, 2, 1), ("R", 7, 2, 0), ("R", 7, 2, 1), ("R", 8, 1, 0),
-    ("R", 8, 1, 1), ("R", 9, 1, 0), ("R", 9, 1, 1), ("A", 4, 1, 0), ("A", 4, 1, 1), ("A", 1, 2, 0), ("T", 2),
-    ("T", 1), ("T", 3), ("T", 0), ("R", 5, 3, 0), ("R", 5, 3, 1), ("R", 6, 3, 0), ("R", 6, 3, 1), ("X", 6),
-    ("R", 7, 3, 0), ("R", 7, 3, 1), ("X", 7), ("A", 5, 0, 0), ("A", 5, 0, 1), ("A", 2, 1, 0), ("A", 2, 1, 1),
-    ("A", 3, 1, 0), ("A", 3, 1, 1), ("A", 1, 2, 1), ("D", 0), ("R", 8, 2, 0), ("R", 8, 2, 1), ("F", 0), ("tr0",),
-    ("tr1",), ("R", 9, 2, 0), ("R", 9, 2, 1), ("A", 4, 2, 0), ("A", 4, 2, 1), ("A", 6, 0, 0), ("A", 6, 0, 1),
-    ("A", 7, 0, 0), ("A", 7, 0, 1), ("A", 5, 1, 1), ("A", 5, 1, 0), ("A", 2, 2, 1), ("A", 2, 2, 0), ("A", 3, 2, 1),
-    ("A", 3, 2, 0), ("D", 1), ("F", 1), ("R", 8, 3, 0), ("R", 8, 3, 1), ("X", 8), ("R", 9, 3, 0), ("R", 9, 3, 1),
-    ("X", 9), ("D", 4), ("F", 4), ("A", 6, 1, 0), ("A", 6, 1, 1), ("A", 8, 0, 0), ("A", 8, 0, 1), ("ts",),
-    ("A", 9, 0, 0), ("A", 9, 0, 1), ("A", 7, 1, 0), ("A", 7, 1, 1), ("A", 5, 2, 0), ("A", 5, 2, 1), ("D", 2),
-    ("D", 3), ("F", 2), ("F", 3), ("A", 6, 2, 0), ("A", 6, 2, 1), ("A", 8, 1, 0), ("A", 8, 1, 1), ("tb",),
-    ("A", 9, 1, 0), ("A", 9, 1, 1), ("A", 7, 2, 0), ("A", 7, 2, 1), ("D", 5), ("nb",), ("F", 5), ("D", 6),
-    ("A", 8, 2, 0), ("A", 8, 2, 1), ("F", 6), ("A", 9, 2, 0), ("A", 9, 2, 1), ("D", 7), ("D", 8), ("F", 7), ("F", 8),
-    ("D", 9), ("F", 9),
+    ("yu", 2), ("yd", 2), ("yf", 4), ("prep", 1), ("qd",), ("qu",), ("wr",), ("P", 1), ("R", 0, 1, 0),
+    ("R", 0, 1, 1), ("yu", 3), ("yd", 3), ("yf", 5), ("P", 2), ("P", 4), ("prep", 2), ("P", 3), ("P", 5),
+    ("R", 1, 1, 0), ("R", 1, 1, 1), ("R", 0, 2, 0), ("R", 0, 2, 1), ("yu", 4), ("yd", 4), ("R", 2, 1, 0),
+    ("R", 2, 1, 1), ("prep", 3), ("P", 6), ("R", 3, 1, 0), ("R", 3, 1, 1), ("R", 4, 1, 0), ("R", 4, 1, 1),
+    ("R", 5, 1, 0), ("R", 5, 1, 1), ("R", 1, 2, 0), ("yu", 5), ("yd", 5), ("R", 1, 2, 1), ("R", 0, 3, 0),
+    ("R", 0, 3, 1), ("A", 0, 0, 0), ("A", 0, 0, 1), ("prep", 4), ("R", 2, 2, 0), ("R", 2, 2, 1), ("R", 6, 1, 0),
+    ("R", 6, 1, 1), ("prep", 5), ("P", 7), ("P", 8), ("P", 9), ("A", 0, 1, 0), ("A", 0, 1, 1), ("R", 3, 2, 0),
+    ("R", 3, 2, 1), ("R", 4, 2, 0), ("R", 4, 2, 1), ("R", 5, 2, 0), ("R", 5, 2, 1), ("R", 6, 2, 0), ("R", 6, 2, 1),
+    ("R", 1, 3, 0), ("R", 1, 3, 1), ("A", 1, 0, 0), ("A", 1, 0, 1), ("R", 7, 1, 0), ("R", 7, 1, 1), ("R", 2, 3, 0),
+    ("R", 2, 3, 1), ("X", 2), ("R", 8, 1, 0), ("R", 8, 1, 1), ("ql",), ("R", 9, 1, 0), ("R", 9, 1, 1), ("P", 10),
+    ("P", 11), ("A", 0, 2, 0), ("A", 0, 2, 1), ("R", 3, 3, 0), ("R", 3, 3, 1), ("X", 3), ("R", 4, 3, 0),
+    ("R", 4, 3, 1), ("X", 4), ("R", 5, 3, 0), ("R", 5, 3, 1), ("X", 5), ("R", 6, 3, 0), ("R", 6, 3, 1),
+    ("A", 6, 0, 0), ("A", 6, 0, 1), ("A", 1, 1, 0), ("A", 1, 1, 1), ("wfu",), ("wfd",), ("R", 7, 2, 0),
+    ("R", 7, 2, 1), ("A", 2, 0, 0), ("A", 2, 0, 1), ("A", 3, 0, 0), ("A", 3, 0, 1), ("A", 4, 0, 0), ("A", 4, 0, 1),
+    ("A", 5, 0, 0), ("A", 5, 0, 1), ("R", 8, 2, 0), ("R", 8, 2, 1), ("R", 9, 2, 0), ("R", 9, 2, 1), ("R", 10, 1, 0),
+    ("R", 10, 1, 1), ("R", 11, 1, 0), ("R", 11, 1, 1), ("D", 0), ("T", 2), ("T", 1), ("T", 3), ("A", 2, 1, 0),
+    ("A", 2, 1, 1), ("A", 3, 1, 0), ("A", 3, 1, 1), ("A", 4, 1, 0), ("A", 4, 1, 1), ("A", 5, 1, 0), ("A", 5, 1, 1),
+    ("A", 6, 1, 0), ("A", 6, 1, 1), ("T", 0), ("A", 1, 2, 0), ("A", 1, 2, 1), ("R", 7, 3, 0), ("R", 7, 3, 1),
+    ("A", 7, 0, 0), ("A", 7, 0, 1), ("R", 8, 3, 0), ("R", 8, 3, 1), ("X", 8), ("R", 9, 3, 0), ("R", 9, 3, 1),
+    ("X", 9), ("F", 0), ("R", 10, 2, 0), ("tr0",), ("tr1",), ("R", 10, 2, 1), ("R", 11, 2, 0), ("R", 11, 2, 1),
+    ("A", 2, 2, 0), ("A", 2, 2, 1), ("A", 3, 2, 0), ("A", 3, 2, 1), ("A", 8, 0, 0), ("A", 8, 0, 1), ("A", 4, 2, 0),
+    ("A", 9, 0, 0), ("A", 9, 0, 1), ("A", 4, 2, 1), ("A", 5, 2, 0), ("A", 5, 2, 1), ("A", 6, 2, 0), ("A", 6, 2, 1),
+    ("D", 1), ("A", 7, 1, 0), ("A", 7, 1, 1), ("F", 1), ("R", 10, 3, 0), ("R", 10, 3, 1), ("X", 10), ("R", 11, 3, 0),
+    ("R", 11, 3, 1), ("X", 11), ("D", 2), ("D", 3), ("F", 2), ("F", 3), ("A", 8, 1, 0), ("A", 8, 1, 1),
+    ("A", 10, 0, 0), ("ts",), ("A", 10, 0, 1), ("A", 11, 0, 0), ("A", 11, 0, 1), ("A", 9, 1, 1), ("A", 9, 1, 0),
+    ("D", 4), ("D", 5), ("F", 4), ("D", 6), ("F", 5), ("A", 7, 2, 0), ("A", 7, 2, 1), ("F", 6), ("A", 8, 2, 0),
+    ("A", 8, 2, 1), ("A", 10, 1, 0), ("A", 10, 1, 1), ("A", 11, 1, 0), ("A", 11, 1, 1), ("A", 9, 2, 0),
+    ("A", 9, 2, 1), ("tb",), ("D", 7), ("F", 7), ("D", 8), ("A", 10, 2, 0), ("A", 10, 2, 1), ("F", 8),
+    ("A", 11, 2, 0), ("A", 11, 2, 1), ("nb",), ("D", 9), ("D", 10), ("F", 9), ("F", 10), ("D", 11), ("F", 11),
 ]
-UNITS = [(0, 0, 1), (0, 1, 1), (1, 0, 2), (3, 0, 2), (0, 2, 2), (0, 4, 2), (1, 2, 4), (3, 2, 4), (2, 0, 3), (2, 3, 3)]
+UNITS = [(0, 0, 1), (0, 1, 1), (1, 0, 1), (3, 0, 1), (1, 1, 1), (3, 1, 1), (0, 2, 2), (0, 4, 2), (1, 2, 4), (3, 2, 4), (2, 0, 3), (2, 3, 3)]
+
+
+def write_out(small, large, small_out, large_out, sem):
+    rows = large.shape[0] // 4
+    copies = [pltpu.make_async_copy(small, small_out, sem.at[4])]
+    for i in range(4):
+        cut = pl.ds(i * rows, rows)
+        copies.append(pltpu.make_async_copy(large.at[cut, :], large_out.at[cut, :], sem.at[i]))
+    for copy in copies:
+        copy.start()
+    for copy in copies:
+        copy.wait()
 
 
 def shards(inputs, norm_gain, norm_bias, query_grad, stream_grad, query_weight):
@@ -412,7 +435,7 @@
     block = width // 8
     vmem = pl.BlockSpec(memory_space=pltpu.VMEM)
     hbm = pl.BlockSpec(memory_space=pltpu.HBM)
-    return pl.pallas_call(
+    results = pl.pallas_call(
         kernel,
         out_shape=(
             pltpu.VMEM((tok, width), BF16),
@@ -454,6 +477,18 @@
             collective_id=0, has_side_effects=True, vmem_limit_bytes=57 * 1024 * 1024
         ),
     )(inputs, norm_gain.reshape(1, width), norm_bias.reshape(1, width), query_grad, stream_grad, query_weight)
+    anywhere = pl.BlockSpec(memory_space=pl.ANY)
+    return pl.pallas_call(
+        write_out,
+        out_shape=(
+            jax.ShapeDtypeStruct((tok, width), BF16),
+            jax.ShapeDtypeStruct((width, cols), BF16),
+        ),
+        in_specs=[anywhere] * 2,
+        out_specs=(hbm, hbm),
+        scratch_shapes=[pltpu.SemaphoreType.DMA((5,))],
+        compiler_params=pltpu.CompilerParams(vmem_limit_bytes=1024 * 1024),
+    )(*[pltpu.with_memory_space_constraint(result, pltpu.VMEM) for result in results])
 
 
 def solution(mesh):

time: 126 us -> 126 us (level)
  local copies, waits for them, and re-layouts: 2.9 us -> 0 us
  Pallas kernels: 123 us -> 125 us
    unnamed x2 -> x0, local copies, waits for them, and re-layouts: 2.9 us -> none
    pallas_call x0 -> x1, Pallas kernels: none -> 2.32 us  [shards(): pl.pallas_call(write_out, out_shape=(jax.ShapeDtypeStruct((tok, width), B...]
where the time goes in v4:
time: 126 us
  Pallas kernels  125 us (99%)
    pallas_call x1, Pallas kernels, shards(): pl.pallas_call(kernel, out_shape=(pltpu.VMEM((tok, width), BF16), pltpu.V...  123 us

profile of v4, /device:TPU:1, one launch (start us, length us, event | category | flops | bytes accessed | tf_op | source)
XLA Modules:
  0.0 126.0 jit_solution(14381987717673359497)
XLA Ops:
  0.6 122.9 %shard_map.77 = (bf16[24,6144]{1,0:T(8,128)(2,1)S(1)}, bf16[6144,384]{1,0:T(8,128)(2,1)S(1)}) custom-call(bf16[24,6144]{1,0:T(8,128)(2,1)} %x_hbm.1, f32[1,6144]{1,0:T(1,128)} %bitcast.2, f32[1,6144]{1,0:T(1,128)} %bitcast.3, bf16[768,384]{1,0:T(8,128)(2,1)} %q_hbm.1, bf16[24,6144]{1,0:T(8,128)(2,1)} %stream_hbm.1, bf16[6144,384]{1,0:T(8,128)(2,1)} %w_ref.1), custom_call_target="tpu_custom_call" | custom-call | tf_op jit(solution)/shard_map/pallas_call | solution.py:438
  123.5 2.3 %shard_map.78 = (bf16[24,6144]{1,0:T(8,128)(2,1)}, bf16[6144,384]{1,0:T(8,128)(2,1)}) custom-call(bf16[24,6144]{1,0:T(8,128)(2,1)S(1)} %get-tuple-element.4.small, bf16[6144,384]{1,0:T(8,128)(2,1)S(1)} %get-tuple-element.5.large), custom_call_target="tpu_custom_call" | custom-call | tf_op jit(solution)/shard_map/pallas_call | solution.py:481
